TPU v7x, 32 devices: a whole 2x2x4 slice. The times are simulated.
32 devices in a mesh: dp: 4 (over z), rows: 8 (over y, x, core).
Axes of the slice: x: 2, y: 2, z: 4, core: 2. Of those that a mesh axis runs over, the one named last changes fastest.
Arguments:
- latent: bfloat16 [8, 8, 64, 640], P('dp', 'rows'), may hold values from -16.25 to 16.25
- hidden: bfloat16 [8, 8, 64, 640], P('dp', 'rows'), may hold values from -16.25 to 16.25
- cotangent: bfloat16 [8, 8, 64, 640], P('dp', 'rows'), may hold values from -6 to 6
- filter_one: bfloat16 [9, 640, 640], P(None, 'dp', 'rows'), may hold values from -0.078125 to 0.078125
- filter_two: bfloat16 [9, 640, 640], P(None, 'dp', 'rows'), may hold values from -0.078125 to 0.078125
- gain_one: float32 [640], replicated, may hold values from 0.1 to 1.9
- shift_one: float32 [640], replicated, may hold values from -2.5 to 2.5
- gain_two: float32 [640], replicated, may hold values from 0.1 to 1.9
- shift_two: float32 [640], replicated, may hold values from -2.5 to 2.5
Outputs:
- latent_grad: bfloat16 [8, 8, 64, 640], P('dp', 'rows')
All inputs are finite; a program needn't handle non-finite values.
Results may differ from a plain program's by a relative error of at most 0.0027.
Values may be sent and summed in bfloat16 or wider, within the bound.
A program may use at most 128 MiB of HBM per device.

v0:
```python
import jax
import jax.numpy as jnp
from jax import lax
from jax.sharding import PartitionSpec as P

GROUPS = 16
GSIZE = 40


def extended(block, sides, width):
    for axis, dim in sides:
        count = lax.axis_size(axis)
        forward = [(i, i + 1) for i in range(count - 1)]
        backward = [(target, source) for source, target in forward]
        low = lax.ppermute(
            lax.slice_in_dim(block, block.shape[dim] - width, None, axis=dim), axis, forward
        )
        high = lax.ppermute(lax.slice_in_dim(block, 0, width, axis=dim), axis, backward)
        block = jnp.concatenate([low, block, high], axis=dim)
    return block


def group_sums(values):
    per_channel = jnp.sum(values, axis=(1, 2))
    return jnp.sum(per_channel.reshape(per_channel.shape[0], GROUPS, -1), axis=2)


def expand_groups(moment):
    return jnp.repeat(moment, GSIZE, axis=1)[:, None, None, :]


def finish_stats(sum_plain, sum_square, number):
    average = sum_plain / number
    variance = sum_square / number - average * average
    return (average, lax.rsqrt(variance + 1e-05))


def reduced_stats(field, number):
    values = field.astype(jnp.float32)
    sum_plain, sum_square = lax.psum((group_sums(values), group_sums(values * values)), "rows")
    return finish_stats(sum_plain, sum_square, number)


def norm_backward(field, stats, gain, shift, incoming, number):
    average, inverse = stats
    values = field.astype(jnp.float32)
    normed = (values - expand_groups(average)) * expand_groups(inverse)
    linear = normed * gain + shift
    logistic = jax.nn.sigmoid(linear)
    scaled = incoming * logistic * (1.0 + linear * (1.0 - logistic)) * gain
    sum_first, sum_second = lax.psum((group_sums(scaled), group_sums(scaled * normed)), "rows")
    first = sum_first / number
    second = sum_second / number
    return expand_groups(inverse) * (scaled - expand_groups(first) - normed * expand_groups(second))


def conv_backward(gradient, weights):
    images, rows_here, breadth, channels = gradient.shape
    padded = extended(gradient, (("rows", 1),), 1)
    padded = jnp.pad(padded, ((0, 0), (0, 0), (1, 1), (0, 0)))
    pixels = images * rows_here * breadth
    shifted = []
    for tap_index in range(9):
        down_step = tap_index // 3 - 1
        side_step = tap_index % 3 - 1
        window = padded[
            :, 1 - down_step : 1 - down_step + rows_here, 1 - side_step : 1 - side_step + breadth, :
        ]
        shifted.append(window.reshape(pixels, channels))
    stacked = jnp.stack(shifted, axis=1)
    gathered = lax.all_gather(weights, "dp", axis=1, tiled=True)
    section = lax.all_gather(gathered, "rows", axis=2, tiled=True)
    columns = section.shape[2]
    window = stacked.reshape(pixels, 9 * columns)
    flat = jnp.transpose(section, (0, 2, 1)).reshape(9 * columns, section.shape[1])
    result = jnp.dot(window, flat, preferred_element_type=jnp.float32)
    return result.reshape(images, rows_here, breadth, channels)


def body(
    latent, hidden, cotangent, filter_one, filter_two, gain_one, shift_one, gain_two, shift_two
):
    number = latent.shape[1] * lax.axis_size("rows") * latent.shape[2] * GSIZE
    stats_two = reduced_stats(hidden, number)
    back_two = conv_backward(cotangent, filter_two)
    hidden_grad = norm_backward(hidden, stats_two, gain_two, shift_two, back_two, number).astype(
        jnp.bfloat16
    )
    stats_one = reduced_stats(latent, number)
    back_one = conv_backward(hidden_grad, filter_one)
    latent_part = norm_backward(latent, stats_one, gain_one, shift_one, back_one, number)
    return (cotangent.astype(jnp.float32) + latent_part).astype(jnp.bfloat16)


def solution(mesh):
    in_specs = (
        P("dp", "rows", None, None),
        P("dp", "rows", None, None),
        P("dp", "rows", None, None),
        P(None, "dp", "rows"),
        P(None, "dp", "rows"),
        P(),
        P(),
        P(),
        P(),
    )
    out_specs = P("dp", "rows", None, None)
    return jax.shard_map(body, mesh=mesh, in_specs=in_specs, out_specs=out_specs, check_vma=False)
```

profile of v0, /device:TPU:0, one launch (start us, length us, event | category | flops | bytes accessed | tf_op | source)
XLA Modules:
  0.0 221.9 jit_solution(1200964164859489196)
XLA Ops:
  6.5 1.2 copy.112
  7.7 47.9 %all_gather.12 = bf16[9,640,80]{2,0,1:T(8,128)(2,1)S(1)} all-gather(bf16[9,160,80]{2,0,1:T(8,128)(2,1)S(1)} %copy.112), channel_id=1, replica_groups=mesh['dp'=4,'rows'=8] {'dp'}, dimensions={1}, use_global_device_ids=true | all-gather | bytes 1152000 | tf_op jit(solution)/shard_map/all_gather | solution.py:71
  55.6 3.0 %copy.113 = bf16[9,640,80]{1,2,0:T(8,128)(2,1)} copy(bf16[9,640,80]{2,0,1:T(8,128)(2,1)S(1)} %all_gather.12) | data formatting | bytes 1843200 | tf_op jit(solution)/shard_map/all_gather | solution.py:71
  58.9 46.2 %all_gather.14 = bf16[9,640,80]{2,0,1:T(8,128)(2,1)S(1)} all-gather(bf16[9,160,80]{2,0,1:T(8,128)(2,1)S(1)} %copy.123), channel_id=1, replica_groups=mesh['dp'=4,'rows'=8] {'dp'}, dimensions={1}, use_global_device_ids=true | all-gather | bytes 1152000 | tf_op jit(solution)/shard_map/all_gather | solution.py:71
  105.1 3.0 %copy.124 = bf16[9,640,80]{1,2,0:T(8,128)(2,1)} copy(bf16[9,640,80]{2,0,1:T(8,128)(2,1)S(1)} %all_gather.14) | data formatting | bytes 1843200 | tf_op jit(solution)/shard_map/all_gather | solution.py:71
  108.2 1.4 collective-permute-start
  109.6 1.3 collective-permute-start.1
  111.3 16.1 %all-reduce.4 = (f32[2,16]{1,0:T(2,128)S(1)}, f32[2,16]{1,0:T(2,128)S(1)}) all-reduce(f32[2,16]{1,0:T(2,128)S(1)} %reduce_sum.151, f32[2,16]{1,0:T(2,128)S(1)} %reduce_sum.149), channel_id=1, replica_groups=mesh['dp'=4,'rows'=8] {'rows'}, use_global_device_ids=true, to_apply=%region_11.12 | all-reduce | flops 64 | bytes 512 | tf_op jit(solution)/shard_map/psum | solution.py:40
  133.9 1.0 copy.104
  135.9 11.1 %stack.6 = bf16[128,9,640]{2,1,0:T(8,128)(2,1)S(1)} concatenate(bf16[128,1,640]{2,1,0:T(2,128)(2,1)S(1)} %copy.103, bf16[128,1,640]{2,1,0:T(2,128)(2,1)} %copy.104, bf16[128,1,640]{2,1,0:T(2,128)(2,1)} %copy.105, bf16[128,1,640]{2,1,0:T(2,128)(2,1)} %copy.106, bf16[128,1,640]{2,1,0:T(2,128)(2,1)S(1)} %copy.107, bf16[128,1,640]{2,1,0:T(2,128)(2,1)} %copy.108, ...), dimensions={1} | concatenate | bytes 2949120 | tf_op jit(solution)/shard_map/stack | solution.py:70
  147.1 1.8 reshape.88
  148.8 5.0 %fusion.53 = (f32[2,640]{1,0:T(2,128)S(1)}, f32[2,640]{1,0:T(2,128)S(1)}, f32[2,1,64,640]{3,2,0,1:T(8,128)S(1)}) fusion(f32[2,640]{1,0:T(2,128)S(1)} %mul.122, f32[2,640]{1,0:T(2,128)S(1)} %sub.60, bf16[2,1,64,640]{3,2,1,0:T(8,128)(2,1)S(1)} %copy-done.4, f32[640]{0:T(1024)S(1)} %copy-done.6, f32[640]{0:T(1024)S(1)} %copy-done.7, ...), kind=kOutput, calls=%fused_computation.73 | convolution fusion | flops 945108480 | bytes 9364480 | tf_op jit(solution)/shard_map/dot_general | solution.py:76
  154.2 12.2 %all-reduce.3 = (f32[2,16]{1,0:T(2,128)S(1)}, f32[2,16]{1,0:T(2,128)S(1)}, f32[2,16]{1,0:T(2,128)S(1)}, f32[2,16]{1,0:T(2,128)S(1)}) all-reduce(f32[2,16]{1,0:T(2,128)S(1)} %reduce_sum.155, f32[2,16]{1,0:T(2,128)S(1)} %reduce_sum.153, f32[2,16]{1,0:T(2,128)S(1)} %reduce_sum.147, ...), channel_id=1, replica_groups=mesh['dp'=4,'rows'=8] {'rows'}, use_global_device_ids=true, to_apply=%region_17.18 | all-reduce | flops 128 | bytes 1024 | tf_op jit(solution)/shard_map/psum | solution.py:51
  166.8 1.7 collective-permute-start.2
  168.5 1.5 collective-permute-start.3
  170.5 1.2 collective-permute-done.3
  172.3 1.0 copy.116
  173.3 1.0 copy.117
  177.3 1.0 copy.115
  178.3 1.0 copy.121
  179.3 11.0 %stack.7 = bf16[128,9,640]{2,1,0:T(8,128)(2,1)S(1)} concatenate(bf16[128,1,640]{2,1,0:T(2,128)(2,1)S(1)} %copy.114, bf16[128,1,640]{2,1,0:T(2,128)(2,1)} %copy.115, bf16[128,1,640]{2,1,0:T(2,128)(2,1)} %copy.116, bf16[128,1,640]{2,1,0:T(2,128)(2,1)} %copy.117, bf16[128,1,640]{2,1,0:T(2,128)(2,1)S(1)} %copy.118, bf16[128,1,640]{2,1,0:T(2,128)(2,1)} %copy.119, ...), dimensions={1} | concatenate | bytes 2949120 | tf_op jit(solution)/shard_map/stack | solution.py:70
  190.3 1.8 reshape.92
  192.1 4.9 %fusion.52 = (f32[2,640]{1,0:T(2,128)S(1)}, f32[2,640]{1,0:T(2,128)S(1)}, f32[2,1,64,640]{3,2,0,1:T(8,128)S(1)}) fusion(f32[2,640]{1,0:T(2,128)S(1)} %mul.118, f32[2,640]{1,0:T(2,128)S(1)} %sub.68, bf16[2,1,64,640]{3,2,1,0:T(8,128)(2,1)S(1)} %copy-done.2, f32[640]{0:T(1024)S(1)} %copy-done.8, f32[640]{0:T(1024)S(1)} %copy-done.9, ...), kind=kOutput, calls=%fused_computation.72 | convolution fusion | flops 945108480 | bytes 9364480 | tf_op jit(solution)/shard_map/dot_general | solution.py:76
  197.5 16.5 %all-reduce.2 = (f32[2,16]{1,0:T(2,128)S(1)}, f32[2,16]{1,0:T(2,128)S(1)}) all-reduce(f32[2,16]{1,0:T(2,128)S(1)} %reduce_sum.159, f32[2,16]{1,0:T(2,128)S(1)} %reduce_sum.157), channel_id=1, replica_groups=mesh['dp'=4,'rows'=8] {'rows'}, use_global_device_ids=true, to_apply=%region_23.24 | all-reduce | flops 64 | bytes 512 | tf_op jit(solution)/shard_map/psum | solution.py:51
  (88 shorter events, 14.5 us)
Async XLA Ops:
  6.5 142.3 %all-gather.3.cloned.1.call-start = ((), (), s32[]{:S(2)}) async-start(), calls=%async_computation | async-start | bytes 8294400 | tf_op jit(solution)/shard_map/all_gather | solution.py:72
  55.6 3.1 %copy-start.5 = (bf16[9,160,80]{2,1,0:T(8,128)(2,1)S(1)}, bf16[9,160,80]{2,1,0:T(8,128)(2,1)}, u32[]{:S(2)}) copy-start(bf16[9,160,80]{2,1,0:T(8,128)(2,1)} %param.12) | copy-start | bytes 691204
  58.7 133.5 %all-gather.5.cloned.1.call-start = ((), (), s32[]{:S(2)}) async-start(), calls=%async_computation.1 | async-start | bytes 8294400 | tf_op jit(solution)/shard_map/all_gather | solution.py:72
  105.1 3.0 %copy-start = (bf16[2,1,64,640]{3,2,1,0:T(8,128)(2,1)S(1)}, bf16[2,1,64,640]{3,2,1,0:T(8,128)(2,1)}, u32[]{:S(2)}) copy-start(bf16[2,1,64,640]{3,2,1,0:T(8,128)(2,1)} %param.11) | copy-start | bytes 491524
  105.1 5.8 %copy-start.3 = (bf16[2,1,64,640]{3,2,1,0:T(8,128)(2,1)S(1)}, bf16[2,1,64,640]{3,2,1,0:T(8,128)(2,1)}, u32[]{:S(2)}) copy-start(bf16[2,1,64,640]{3,2,1,0:T(8,128)(2,1)} %param.10) | copy-start | bytes 491524
  108.1 19.9 %copy-start.1 = (bf16[2,1,64,640]{3,2,1,0:T(8,128)(2,1)S(1)}, bf16[2,1,64,640]{3,2,1,0:T(8,128)(2,1)}, u32[]{:S(2)}) copy-start(bf16[2,1,64,640]{3,2,1,0:T(8,128)(2,1)} %param.9) | copy-start | bytes 491524
  108.2 20.3 %collective-permute-start = (bf16[2,1,64,640]{3,2,1,0:T(8,128)(2,1)S(1)}, bf16[2,1,64,640]{3,2,1,0:T(8,128)(2,1)S(1)}, u32[]{:S(2)}, u32[]{:S(2)}) collective-permute-start(bf16[2,1,64,640]{3,2,1,0:T(8,128)(2,1)S(1)} %copy-done), channel_id=1, source_target_pairs={{0,1},{1,2},{2,3},{3,4},{4,5},{5,6},{6,7},{8,9},{9,10},{10,11},{11... | collective-permute-start | bytes 491528 | tf_op jit(solution)/shard_map/ppermute | solution.py:15
  109.6 18.8 %collective-permute-start.1 = (bf16[2,1,64,640]{3,2,1,0:T(8,128)(2,1)S(1)}, bf16[2,1,64,640]{3,2,1,0:T(8,128)(2,1)S(1)}, u32[]{:S(2)}, u32[]{:S(2)}) collective-permute-start(bf16[2,1,64,640]{3,2,1,0:T(8,128)(2,1)S(1)} %copy-done), channel_id=1, source_target_pairs={{1,0},{2,1},{3,2},{4,3},{5,4},{6,5},{7,6},{9,8},{10,9},{11,10},{12... | collective-permute-start | bytes 491528 | tf_op jit(solution)/shard_map/ppermute | solution.py:18
  147.0 1.8 copy-start.4
  147.0 1.8 copy-start.6
  147.0 1.8 copy-start.7
  166.8 3.8 %collective-permute-start.2 = (bf16[2,1,64,640]{3,2,0,1:T(8,128)(2,1)S(1)}, bf16[2,1,64,640]{3,2,0,1:T(8,128)(2,1)S(1)}, u32[]{:S(2)}, u32[]{:S(2)}) collective-permute-start(bf16[2,1,64,640]{3,2,0,1:T(8,128)(2,1)S(1)} %fusion.50), channel_id=1, source_target_pairs={{0,1},{1,2},{2,3},{3,4},{4,5},{5,6},{6,7},{8,9},{9,10},{10,11},{11... | collective-permute-start | bytes 491528 | tf_op jit(solution)/shard_map/ppermute | solution.py:15
  168.5 3.3 %collective-permute-start.3 = (bf16[2,1,64,640]{3,2,0,1:T(8,128)(2,1)S(1)}, bf16[2,1,64,640]{3,2,0,1:T(8,128)(2,1)S(1)}, u32[]{:S(2)}, u32[]{:S(2)}) collective-permute-start(bf16[2,1,64,640]{3,2,0,1:T(8,128)(2,1)S(1)} %fusion.50), channel_id=1, source_target_pairs={{1,0},{2,1},{3,2},{4,3},{5,4},{6,5},{7,6},{9,8},{10,9},{11,10},{12... | collective-permute-start | bytes 491528 | tf_op jit(solution)/shard_map/ppermute | solution.py:18
  190.3 1.8 copy-start.2
  190.3 1.8 copy-start.8
  190.3 1.8 copy-start.9
Sparse Core Ops, SparseCore 0:
  58.8 51.7 all-gather.2
  112.5 50.0 all-gather.4
where the time goes:
time: 225 us; the launch traced here: 222 us
  blocking collectives  139 us (62%)
  local copies, waits for them, and re-layouts  50.2 us (22%)
  between operations  13.8 us (6%)
  matrix products  9.93 us (4%)
  starting transfers between devices  5.91 us (3%)
    all_gather x2, blocking collectives, conv_backward(): gathered = lax.all_gather(weights, 'dp', axis=1, tiled=True)  94.1 us
    another operation x20, local copies, waits for them, and re-layouts, conv_backward(): stacked = jnp.stack(shifted, axis=1)  36.9 us
    psum x2, blocking collectives, norm_backward(): lax.psum((group_sums(scaled), group_sums(scaled * normed)), 'rows')  28.7 us
    psum x1, blocking collectives, reduced_stats(): lax.psum((group_sums(values), group_sums(values * values)), 'rows')  16.1 us
    dot_general x2, matrix products, conv_backward(): result = jnp.dot(window, flat, preferred_element_type=jnp.float32)  9.93 us
    all_gather x2, local copies, waits for them, and re-layouts, conv_backward(): gathered = lax.all_gather(weights, 'dp', axis=1, tiled=True)  5.97 us
  transfers between devices with their start and end apart: 6, of which 1 were waited for; matrix products, arithmetic and copies ran while one was open for 23% of the time, Pallas kernels for 0%

commit v1 on v0

--- a/solution.py
+++ b/solution.py
@@ -1,10 +1,16 @@
+import functools
+
 import jax
 import jax.numpy as jnp
 from jax import lax
+from jax.experimental import pallas as pl
+from jax.experimental.pallas import tpu as pltpu
 from jax.sharding import PartitionSpec as P
 
 GROUPS = 16
 GSIZE = 40
+TAPS = 9
+MESH = pl.DeviceIdType.MESH
 
 
 def extended(block, sides, width):
@@ -77,7 +83,7 @@
     return result.reshape(images, rows_here, breadth, channels)
 
 
-def body(
+def plain_body(
     latent, hidden, cotangent, filter_one, filter_two, gain_one, shift_one, gain_two, shift_two
 ):
     number = latent.shape[1] * lax.axis_size("rows") * latent.shape[2] * GSIZE
@@ -92,7 +98,307 @@
     return (cotangent.astype(jnp.float32) + latent_part).astype(jnp.bfloat16)
 
 
+def kernel(
+    depth, rows, breadth,
+    lat_ref, hid_ref, cot_ref, f1_ref, f2_ref, par_ref,
+    out_ref,
+    x_cot, x_hg, lat_t, hid_t, lat_b, hid_b, stage1, stage2, w1, w2, wt, y_ref, back, out_b, out_t,
+    z_send, z_recv, w_send, w_recv, c_send, c_recv, g_send, g_recv,
+    a_send, a_recv, o_send, o_recv,
+):
+    d = lax.axis_index("dp")
+    r = lax.axis_index("rows")
+    channels, lanes = x_cot.shape[1:]
+    block = channels // rows
+    images = lanes // breadth
+    halves = rows // depth
+    wide = w1.shape[2]
+    number = rows * breadth * GSIZE
+
+    def remote(src, dst, send, recv, **device):
+        return pltpu.make_async_remote_copy(
+            src_ref=src, dst_ref=dst, send_sem=send, recv_sem=recv,
+            device_id=device, device_id_type=MESH,
+        )
+
+    barrier = pltpu.get_barrier_semaphore()
+    for off in range(1, depth):
+        pl.semaphore_signal(barrier, inc=1, device_id={"dp": lax.rem(d + off, depth)}, device_id_type=MESH)
+    for off in range(1, rows):
+        pl.semaphore_signal(barrier, inc=1, device_id={"rows": lax.rem(r + off, rows)}, device_id_type=MESH)
+
+    x_cot[r] = cot_ref[...].T
+    hid_t[...] = hid_ref[...].T
+    lat_t[...] = lat_ref[...].T
+    pl.semaphore_wait(barrier, depth - 1 + rows - 1)
+
+    pending = []
+
+    def start_z(which, src, stage):
+        for off in (2, 1, 3) if depth == 4 else range(1, depth):
+            to = lax.rem(d + off, depth)
+            copy = remote(src, stage.at[d], z_send.at[which, to], z_recv.at[which, d], dp=to)
+            copy.start()
+            pending.append(copy)
+
+    def start_exchange(which, src, dst):
+        for off in range(1, rows):
+            to = lax.rem(r + off, rows)
+            copy = remote(
+                src.at[pl.ds(to * block, block), :], dst.at[r],
+                a_send.at[which, to], a_recv.at[which, r], rows=to,
+            )
+            copy.start()
+            pending.append(copy)
+        dst[r] = src[pl.ds(pl.multiple_of(r * block, block), block), :]
+
+    def wait_exchange(which, src, dst):
+        for off in range(1, rows):
+            frm = lax.rem(r + off, rows)
+            remote(src.at[pl.ds(0, block), :], dst.at[frm], a_send.at[which, frm], a_recv.at[which, frm], rows=frm).wait_recv()
+
+    def send_pieces(which, origin, get, w, wait_own):
+        for k in range(halves):
+            to = origin * halves + k
+
+            @pl.when(to != r)
+            def _():
+                remote(get(k), w.at[r], w_send.at[which, to], w_recv.at[which, r], rows=to).start()
+
+            @pl.when(to == r)
+            def _():
+                w[r] = get(k)[...]
+
+    def wait_piece_sends(which, src, w):
+        for off in range(1, rows):
+            to = lax.rem(r + off, rows)
+            remote(src.at[0], w.at[r], w_send.at[which, to], w_recv.at[which, r], rows=to).wait_send()
+
+    def relay_filters(which, stage, w):
+        for off in (1, 3, 2) if depth == 4 else range(1, depth):
+            origin = lax.rem(d + off, depth)
+            remote(stage.at[origin], stage.at[origin], z_send.at[which, origin], z_recv.at[which, origin], dp=origin).wait_recv()
+            send_pieces(which, origin, lambda k: stage.at[origin, k], w, False)
+
+    def wait_filters(which, src, w):
+        for off in range(1, rows):
+            frm = lax.rem(r + off, rows)
+            remote(src.at[0], w.at[frm], w_send.at[which, frm], w_recv.at[which, frm], rows=frm).wait_recv()
+
+    parity = lax.rem(r, 2)
+    sibling = r + 1 - 2 * parity
+
+    def gather_send(at, send, recv):
+        for off in range(1, rows // 2):
+            to = lax.rem(r + 2 * off, rows)
+            copy = remote(at(r), at(r), send.at[to], recv.at[r], rows=to)
+            copy.start()
+            pending.append(copy)
+        copy = remote(at(r), at(r), send.at[sibling], recv.at[r], rows=sibling)
+        copy.start()
+        pending.append(copy)
+
+    def gather_relay(at, send, recv):
+        for off in range(1, rows // 2):
+            frm = lax.rem(r + 2 * off, rows)
+            remote(at(frm), at(frm), send.at[frm], recv.at[frm], rows=frm).wait_recv()
+            twin = lax.rem(sibling + 2 * off, rows)
+            copy = remote(at(frm), at(frm), send.at[twin], recv.at[frm], rows=sibling)
+            copy.start()
+            pending.append(copy)
+
+    def gather_wait(at, send, recv):
+        for off in range(0, rows // 2):
+            frm = lax.rem(sibling + 2 * off, rows)
+            remote(at(frm), at(frm), send.at[frm], recv.at[frm], rows=sibling).wait_recv()
+
+    def cot_at(h):
+        return x_cot.at[h]
+
+    def hg_at(owner):
+        return x_hg.at[:, pl.ds(pl.multiple_of(owner * block, block), block), :]
+
+    start_z(0, f2_ref, stage2)
+    gather_send(cot_at, c_send, c_recv)
+    start_exchange(0, hid_t, hid_b)
+    send_pieces(0, d, lambda k: f2_ref.at[k], w2, True)
+    start_z(1, f1_ref, stage1)
+    start_exchange(1, lat_t, lat_b)
+
+    lane = lax.broadcasted_iota(jnp.int32, (1, lanes), 1)
+    column = lax.rem(lane, breadth)
+    image_of = lax.div(lane, breadth)
+    groups = block // GSIZE
+
+    def group_means(sums):
+        per_lane = jnp.sum(sums.reshape(groups, GSIZE, lanes), axis=1)
+        total = jnp.zeros_like(per_lane)
+        for image in range(images):
+            mine = image_of == image
+            part = jnp.sum(jnp.where(mine, per_lane, 0.0), axis=1, keepdims=True)
+            total = jnp.where(mine, part, total)
+        total = total * (1.0 / number)
+        return jnp.broadcast_to(total[:, None, :], (groups, GSIZE, lanes)).reshape(block, lanes)
+
+    def stats(field):
+        plain = jnp.zeros((block, lanes), jnp.float32)
+        square = jnp.zeros((block, lanes), jnp.float32)
+        for h in range(rows):
+            values = field[h].astype(jnp.float32)
+            plain += values
+            square += values * values
+        average = group_means(plain)
+        variance = group_means(square) - average * average
+        return average, lax.rsqrt(variance + 1e-05)
+
+    params = par_ref[pl.ds(pl.multiple_of(r * block, block), block), :]
+
+    def conv(x, w):
+        wt[...] = w[...].reshape(channels, wide).T
+        for h in range(0, rows, 2):
+            pair = jnp.concatenate([x[h], x[h + 1]], axis=1)
+            result = jnp.dot(wt[...], pair, preferred_element_type=jnp.float32)
+            y_ref[h] = result[:, :lanes]
+            y_ref[h + 1] = result[:, lanes:]
+
+    def back_at(h):
+        sums = []
+        for side in range(3):
+            total = None
+            for down in range(3):
+                source = h - (down - 1)
+                if 0 <= source < rows:
+                    tap = 3 * down + side
+                    term = y_ref[source, tap * block : (tap + 1) * block, :]
+                    total = term if total is None else total + term
+            sums.append(total)
+        left = jnp.where(column == breadth - 1, 0.0, pltpu.roll(sums[0], lanes - 1, 1))
+        right = jnp.where(column == 0, 0.0, pltpu.roll(sums[2], 1, 1))
+        return sums[1] + left + right
+
+    def norm(field, moments, gain, shift, finish):
+        average, inverse = moments
+        sum_first = jnp.zeros((block, lanes), jnp.float32)
+        sum_second = jnp.zeros((block, lanes), jnp.float32)
+        for h in range(rows):
+            normed = (field[h].astype(jnp.float32) - average) * inverse
+            linear = normed * gain + shift
+            logistic = 1.0 / (1.0 + jnp.exp(-linear))
+            scaled = back_at(h) * logistic * (1.0 + linear * (1.0 - logistic)) * gain
+            back[h] = scaled
+            sum_first += scaled
+            sum_second += scaled * normed
+        first = group_means(sum_first)
+        second = group_means(sum_second)
+        for h in range(rows):
+            normed = (field[h].astype(jnp.float32) - average) * inverse
+            finish(h, inverse * (back[h] - first - normed * second))
+
+    gather_relay(cot_at, c_send, c_recv)
+    wait_exchange(0, hid_t, hid_b)
+    moments_two = stats(hid_b)
+    relay_filters(0, stage2, w2)
+    send_pieces(1, d, lambda k: f1_ref.at[k], w1, True)
+    wait_exchange(1, lat_t, lat_b)
+    moments_one = stats(lat_b)
+    gather_wait(cot_at, c_send, c_recv)
+    wait_filters(0, f2_ref, w2)
+
+    conv(x_cot, w2)
+    mine = pl.ds(pl.multiple_of(r * block, block), block)
+
+    def finish_two(h, value):
+        x_hg[h, mine, :] = value.astype(jnp.bfloat16)
+
+    norm(hid_b, moments_two, params[:, 2:3], params[:, 3:4], finish_two)
+    gather_send(hg_at, g_send, g_recv)
+    gather_relay(hg_at, g_send, g_recv)
+    relay_filters(1, stage1, w1)
+    gather_wait(hg_at, g_send, g_recv)
+    wait_filters(1, f1_ref, w1)
+
+    conv(x_hg, w1)
+
+    def finish_one(h, value):
+        out_b[h] = (x_cot[h, mine, :].astype(jnp.float32) + value).astype(jnp.bfloat16)
+
+    norm(lat_b, moments_one, params[:, 0:1], params[:, 1:2], finish_one)
+    for off in range(1, rows):
+        to = lax.rem(r + off, rows)
+        copy = remote(out_b.at[to], out_t.at[r], o_send.at[to], o_recv.at[r], rows=to)
+        copy.start()
+        pending.append(copy)
+    out_t[r] = out_b[r]
+    for off in range(1, rows):
+        frm = lax.rem(r + off, rows)
+        remote(out_b.at[frm], out_t.at[frm], o_send.at[frm], o_recv.at[frm], rows=frm).wait_recv()
+    out_ref[...] = out_t[...].reshape(channels, lanes).T
+    for copy in pending:
+        copy.wait_send()
+    wait_piece_sends(0, f2_ref, w2)
+    wait_piece_sends(1, f1_ref, w1)
+
+
+def arranged(weights, depth, rows):
+    taps, inner, outer = weights.shape
+    halves = rows // depth
+    cut = weights.reshape(taps, halves, inner // halves, outer)
+    flat = jnp.transpose(cut, (1, 3, 0, 2)).reshape(halves, outer, taps * (inner // halves))
+    return jnp.pad(flat, ((0, 0), (0, 0), (0, -flat.shape[2] % 128)))
+
+
+def kernel_body(
+    depth, rows,
+    latent, hidden, cotangent, filter_one, filter_two, gain_one, shift_one, gain_two, shift_two,
+):
+    images, _, breadth, channels = latent.shape
+    lanes = images * breadth
+    block = channels // rows
+    halves = rows // depth
+    f1 = arranged(filter_one, depth, rows)
+    f2 = arranged(filter_two, depth, rows)
+    wide = f1.shape[2]
+    params = jnp.stack([gain_one, shift_one, gain_two, shift_two], axis=1)
+    bf16, f32 = jnp.bfloat16, jnp.float32
+    dma = pltpu.SemaphoreType.DMA
+    out = pl.pallas_call(
+        functools.partial(kernel, depth, rows, breadth),
+        out_shape=jax.ShapeDtypeStruct((lanes, channels), bf16),
+        in_specs=[pl.BlockSpec(memory_space=pltpu.VMEM)] * 6,
+        out_specs=pl.BlockSpec(memory_space=pltpu.VMEM),
+        scratch_shapes=[
+            pltpu.VMEM((rows, channels, lanes), bf16),
+            pltpu.VMEM((rows, channels, lanes), bf16),
+            pltpu.VMEM((channels, lanes), bf16),
+            pltpu.VMEM((channels, lanes), bf16),
+            pltpu.VMEM((rows, block, lanes), bf16),
+            pltpu.VMEM((rows, block, lanes), bf16),
+            pltpu.VMEM((depth, halves, block, wide), bf16),
+            pltpu.VMEM((depth, halves, block, wide), bf16),
+            pltpu.VMEM((rows, block, wide), bf16),
+            pltpu.VMEM((rows, block, wide), bf16),
+            pltpu.VMEM((wide, channels), bf16),
+            pltpu.VMEM((rows, wide, lanes), f32),
+            pltpu.VMEM((rows, block, lanes), f32),
+            pltpu.VMEM((rows, block, lanes), bf16),
+            pltpu.VMEM((rows, block, lanes), bf16),
+            dma((2, depth)), dma((2, depth)),
+            dma((2, rows)), dma((2, rows)),
+            dma((rows,)), dma((rows,)),
+            dma((rows,)), dma((rows,)),
+            dma((2, rows)), dma((2, rows)),
+            dma((rows,)), dma((rows,)),
+        ],
+        compiler_params=pltpu.CompilerParams(collective_id=0, has_side_effects=True),
+    )(
+        latent.reshape(lanes, channels), hidden.reshape(lanes, channels),
+        cotangent.reshape(lanes, channels), f1, f2, params,
+    )
+    return out.reshape(latent.shape)
+
+
 def solution(mesh):
+    depth, rows = mesh.shape["dp"], mesh.shape["rows"]
     in_specs = (
         P("dp", "rows", None, None),
         P("dp", "rows", None, None),
@@ -104,5 +410,21 @@
         P(),
         P(),
     )
-    out_specs = P("dp", "rows", None, None)
-    return jax.shard_map(body, mesh=mesh, in_specs=in_specs, out_specs=out_specs, check_vma=False)
+
+    def body(latent, *rest):
+        images, rows_here, breadth, channels = latent.shape
+        fits = (
+            rows_here == 1
+            and images * breadth == 128
+            and rows % (2 * depth) == 0
+            and channels % (rows * GSIZE) == 0
+            and (channels // rows) % 16 == 0
+            and channels % 128 == 0
+        )
+        if fits:
+            return kernel_body(depth, rows, latent, *rest)
+        return plain_body(latent, *rest)
+
+    return jax.shard_map(
+        body, mesh=mesh, in_specs=in_specs, out_specs=P("dp", "rows", None, None), check_vma=False
+    )

time: 225 us -> 86.5 us (0.38)
  the two profiles are of different devices: /device:TPU:0 before, /device:TPU:15 now
where the time goes in v1:
time: 86.5 us; the launch traced here: 86.2 us
  Pallas kernels  78.4 us (91%)
  local copies, waits for them, and re-layouts  7.72 us (9%)
    pallas_call x1, Pallas kernels, kernel_body(): pl.pallas_call(functools.partial(kernel, depth, rows, breadth), out_shape...  78.4 us
    unnamed x11, local copies, waits for them, and re-layouts  4 us

profile of v1, /device:TPU:15, one launch (start us, length us, event | category | flops | bytes accessed | tf_op | source)
XLA Modules:
  0.0 86.2 jit_solution(8975911413438524719)
XLA Ops:
  0.0 1.0 %copy.22 = bf16[9,2,80,80]{3,2,0,1:T(8,128)(2,1)S(1)} copy(bf16[9,2,80,80]{3,2,1,0:T(8,128)(2,1)} %bitcast.17) | data formatting | bytes 460800 | tf_op jit(solution)/shard_map/reshape | solution.py:345
  1.0 0.2 copy.23
  1.2 0.0 copy-start
  1.2 0.7 pad.7.f1_ref
  1.9 0.3 copy-done
  2.3 0.2 copy.25
  2.5 0.0 copy-start.1
  2.5 0.7 pad.8.f2_ref
  3.2 0.0 copy-done.1
  3.2 0.0 copy-start.2
  3.2 0.7 copy-done.2
  3.9 0.0 copy-start.3
  3.9 0.7 copy-done.3
  4.6 0.0 copy-start.4
  4.6 0.7 copy-done.4
  5.3 0.9 %copy.26.par_ref = f32[640,4]{1,0:T(8,128)} copy(f32[640,4]{0,1:T(4,128)S(1)} %pad_maximum_fusion) | data formatting | bytes 20480 | tf_op jit(solution)/shard_map/stack | solution.py:361
  6.2 78.4 %shard_map.91 = bf16[128,640]{1,0:T(8,128)(2,1)} custom-call(bf16[128,640]{1,0:T(8,128)(2,1)} %bitcast.19, bf16[128,640]{1,0:T(8,128)(2,1)} %bitcast.20, bf16[128,640]{1,0:T(8,128)(2,1)} %bitcast.21, bf16[2,80,768]{2,1,0:T(8,128)(2,1)} %pad.7.f1_ref, bf16[2,80,768]{2,1,0:T(8,128)(2,1)} %pad.8.f2_ref, f32[640,4]{1,0:T(8,128)} %copy.26.par_ref), custom_call_target="tpu_custom_call" | custom-call | tf_op jit(solution)/shard_map/pallas_call | solution.py:364
  84.6 1.6 %copy.29 = bf16[2,1,64,640]{3,2,1,0:T(8,128)(2,1)} copy(bf16[2,1,64,640]{3,2,1,0:T(8,128)(2,1)} %bitcast.16) | data formatting | bytes 327680
  (6 shorter events, 0.1 us)
Async XLA Ops:
  1.2 1.1 %copy-start = (bf16[9,160,80]{2,1,0:T(8,128)(2,1)S(1)}, bf16[9,160,80]{2,1,0:T(8,128)(2,1)}, u32[]{:S(2)}) copy-start(bf16[9,160,80]{2,1,0:T(8,128)(2,1)} %param.13) | copy-start | bytes 691204
  2.5 0.7 copy-start.1
  3.2 0.7 copy-start.2
  3.9 0.7 copy-start.3
  4.6 0.7 copy-start.4

commit v2 on v1

--- a/solution.py
+++ b/solution.py
@@ -100,9 +100,10 @@
 
 def kernel(
     depth, rows, breadth,
-    lat_ref, hid_ref, cot_ref, f1_ref, f2_ref, par_ref,
+    lat_ref, hid_ref, cot_ref, raw1, raw2, gain1, shift1, gain2, shift2,
     out_ref,
     x_cot, x_hg, lat_t, hid_t, lat_b, hid_b, stage1, stage2, w1, w2, wt, y_ref, back, out_b, out_t,
+    f1_ref, f2_ref, par_ref,
     z_send, z_recv, w_send, w_recv, c_send, c_recv, g_send, g_recv,
     a_send, a_recv, o_send, o_recv,
 ):
@@ -115,6 +116,20 @@
     wide = w1.shape[2]
     number = rows * breadth * GSIZE
 
+    def place(index):
+        return index + lax.rem(index, 2) * (rows - 2 * index)
+
+    def rows_of(index):
+        return pl.ds(pl.multiple_of(place(index) * block, block), block)
+
+    def arrange(raw, ready):
+        for k in range(halves):
+            ready[k, :, TAPS * block :] = jnp.zeros((block, wide - TAPS * block), jnp.bfloat16)
+        for tap in range(TAPS):
+            turned = raw[tap].T
+            for k in range(halves):
+                ready[k, :, tap * block : (tap + 1) * block] = turned[:, k * block : (k + 1) * block]
+
     def remote(src, dst, send, recv, **device):
         return pltpu.make_async_remote_copy(
             src_ref=src, dst_ref=dst, send_sem=send, recv_sem=recv,
@@ -127,6 +142,7 @@
     for off in range(1, rows):
         pl.semaphore_signal(barrier, inc=1, device_id={"rows": lax.rem(r + off, rows)}, device_id_type=MESH)
 
+    arrange(raw2, f2_ref)
     x_cot[r] = cot_ref[...].T
     hid_t[...] = hid_ref[...].T
     lat_t[...] = lat_ref[...].T
@@ -134,23 +150,39 @@
 
     pending = []
 
+    def z_hop(which, src, stage, origin, way):
+        to = d + 1 - 2 * way
+        return remote(src, stage.at[origin], z_send.at[which, way, origin], z_recv.at[which, origin], dp=to)
+
     def start_z(which, src, stage):
-        for off in (2, 1, 3) if depth == 4 else range(1, depth):
-            to = lax.rem(d + off, depth)
-            copy = remote(src, stage.at[d], z_send.at[which, to], z_recv.at[which, d], dp=to)
-            copy.start()
-            pending.append(copy)
+        @pl.when(d < depth - 1)
+        def _():
+            z_hop(which, src, stage, d, 0).start()
+
+        @pl.when(d > 0)
+        def _():
+            z_hop(which, src, stage, d, 1).start()
+
+    def wait_z_sends(which, src, stage):
+        for origin in range(depth):
+            @pl.when((d < depth - 1) & (origin <= d))
+            def _():
+                z_hop(which, src, stage, origin, 0).wait_send()
+
+            @pl.when((d > 0) & (origin >= d))
+            def _():
+                z_hop(which, src, stage, origin, 1).wait_send()
 
     def start_exchange(which, src, dst):
         for off in range(1, rows):
             to = lax.rem(r + off, rows)
             copy = remote(
-                src.at[pl.ds(to * block, block), :], dst.at[r],
+                src.at[rows_of(to), :], dst.at[r],
                 a_send.at[which, to], a_recv.at[which, r], rows=to,
             )
             copy.start()
             pending.append(copy)
-        dst[r] = src[pl.ds(pl.multiple_of(r * block, block), block), :]
+        dst[r] = src[rows_of(r), :]
 
     def wait_exchange(which, src, dst):
         for off in range(1, rows):
@@ -159,7 +191,7 @@
 
     def send_pieces(which, origin, get, w, wait_own):
         for k in range(halves):
-            to = origin * halves + k
+            to = place(origin * halves + k)
 
             @pl.when(to != r)
             def _():
@@ -174,10 +206,29 @@
             to = lax.rem(r + off, rows)
             remote(src.at[0], w.at[r], w_send.at[which, to], w_recv.at[which, r], rows=to).wait_send()
 
-    def relay_filters(which, stage, w):
-        for off in (1, 3, 2) if depth == 4 else range(1, depth):
-            origin = lax.rem(d + off, depth)
-            remote(stage.at[origin], stage.at[origin], z_send.at[which, origin], z_recv.at[which, origin], dp=origin).wait_recv()
+    def relay_filters(which, stage, w, off):
+        @pl.when(d >= off)
+        def _():
+            origin = d - off
+            hop = z_hop(which, stage.at[origin], stage, origin, 0)
+            hop.wait_recv()
+
+            @pl.when(d < depth - 1)
+            def _():
+                hop.start()
+
+            send_pieces(which, origin, lambda k: stage.at[origin, k], w, False)
+
+        @pl.when(d + off < depth)
+        def _():
+            origin = d + off
+            hop = z_hop(which, stage.at[origin], stage, origin, 1)
+            hop.wait_recv()
+
+            @pl.when(d > 0)
+            def _():
+                hop.start()
+
             send_pieces(which, origin, lambda k: stage.at[origin, k], w, False)
 
     def wait_filters(which, src, w):
@@ -216,14 +267,16 @@
         return x_cot.at[h]
 
     def hg_at(owner):
-        return x_hg.at[:, pl.ds(pl.multiple_of(owner * block, block), block), :]
+        return x_hg.at[:, rows_of(owner), :]
 
     start_z(0, f2_ref, stage2)
     gather_send(cot_at, c_send, c_recv)
     start_exchange(0, hid_t, hid_b)
     send_pieces(0, d, lambda k: f2_ref.at[k], w2, True)
-    start_z(1, f1_ref, stage1)
     start_exchange(1, lat_t, lat_b)
+    arrange(raw1, f1_ref)
+    raw_params = [gain1[...], shift1[...], gain2[...], shift2[...]]
+    par_ref[...] = jnp.concatenate(raw_params + raw_params, axis=0).T
 
     lane = lax.broadcasted_iota(jnp.int32, (1, lanes), 1)
     column = lax.rem(lane, breadth)
@@ -251,7 +304,7 @@
         variance = group_means(square) - average * average
         return average, lax.rsqrt(variance + 1e-05)
 
-    params = par_ref[pl.ds(pl.multiple_of(r * block, block), block), :]
+    params = par_ref[rows_of(r), :]
 
     def conv(x, w):
         wt[...] = w[...].reshape(channels, wide).T
@@ -295,25 +348,30 @@
             finish(h, inverse * (back[h] - first - normed * second))
 
     gather_relay(cot_at, c_send, c_recv)
+    relay_filters(0, stage2, w2, 1)
     wait_exchange(0, hid_t, hid_b)
     moments_two = stats(hid_b)
-    relay_filters(0, stage2, w2)
-    send_pieces(1, d, lambda k: f1_ref.at[k], w1, True)
     wait_exchange(1, lat_t, lat_b)
     moments_one = stats(lat_b)
+    for off in range(2, depth):
+        relay_filters(0, stage2, w2, off)
+    start_z(1, f1_ref, stage1)
     gather_wait(cot_at, c_send, c_recv)
     wait_filters(0, f2_ref, w2)
 
     conv(x_cot, w2)
-    mine = pl.ds(pl.multiple_of(r * block, block), block)
+    mine = rows_of(r)
 
     def finish_two(h, value):
         x_hg[h, mine, :] = value.astype(jnp.bfloat16)
 
     norm(hid_b, moments_two, params[:, 2:3], params[:, 3:4], finish_two)
     gather_send(hg_at, g_send, g_recv)
+    send_pieces(1, d, lambda k: f1_ref.at[k], w1, True)
+    relay_filters(1, stage1, w1, 1)
     gather_relay(hg_at, g_send, g_recv)
-    relay_filters(1, stage1, w1)
+    for off in range(2, depth):
+        relay_filters(1, stage1, w1, off)
     gather_wait(hg_at, g_send, g_recv)
     wait_filters(1, f1_ref, w1)
 
@@ -325,26 +383,20 @@
     norm(lat_b, moments_one, params[:, 0:1], params[:, 1:2], finish_one)
     for off in range(1, rows):
         to = lax.rem(r + off, rows)
-        copy = remote(out_b.at[to], out_t.at[r], o_send.at[to], o_recv.at[r], rows=to)
+        copy = remote(out_b.at[to], out_t.at[place(r)], o_send.at[to], o_recv.at[r], rows=to)
         copy.start()
         pending.append(copy)
-    out_t[r] = out_b[r]
+    out_t[place(r)] = out_b[r]
     for off in range(1, rows):
         frm = lax.rem(r + off, rows)
-        remote(out_b.at[frm], out_t.at[frm], o_send.at[frm], o_recv.at[frm], rows=frm).wait_recv()
+        remote(out_b.at[frm], out_t.at[place(frm)], o_send.at[frm], o_recv.at[frm], rows=frm).wait_recv()
     out_ref[...] = out_t[...].reshape(channels, lanes).T
     for copy in pending:
         copy.wait_send()
+    wait_z_sends(0, f2_ref, stage2)
+    wait_z_sends(1, f1_ref, stage1)
     wait_piece_sends(0, f2_ref, w2)
     wait_piece_sends(1, f1_ref, w1)
-
-
-def arranged(weights, depth, rows):
-    taps, inner, outer = weights.shape
-    halves = rows // depth
-    cut = weights.reshape(taps, halves, inner // halves, outer)
-    flat = jnp.transpose(cut, (1, 3, 0, 2)).reshape(halves, outer, taps * (inner // halves))
-    return jnp.pad(flat, ((0, 0), (0, 0), (0, -flat.shape[2] % 128)))
 
 
 def kernel_body(
@@ -355,16 +407,13 @@
     lanes = images * breadth
     block = channels // rows
     halves = rows // depth
-    f1 = arranged(filter_one, depth, rows)
-    f2 = arranged(filter_two, depth, rows)
-    wide = f1.shape[2]
-    params = jnp.stack([gain_one, shift_one, gain_two, shift_two], axis=1)
+    wide = -(-TAPS * block // 128) * 128
     bf16, f32 = jnp.bfloat16, jnp.float32
     dma = pltpu.SemaphoreType.DMA
     out = pl.pallas_call(
         functools.partial(kernel, depth, rows, breadth),
         out_shape=jax.ShapeDtypeStruct((lanes, channels), bf16),
-        in_specs=[pl.BlockSpec(memory_space=pltpu.VMEM)] * 6,
+        in_specs=[pl.BlockSpec(memory_space=pltpu.VMEM)] * 9,
         out_specs=pl.BlockSpec(memory_space=pltpu.VMEM),
         scratch_shapes=[
             pltpu.VMEM((rows, channels, lanes), bf16),
@@ -382,7 +431,10 @@
             pltpu.VMEM((rows, block, lanes), f32),
             pltpu.VMEM((rows, block, lanes), bf16),
             pltpu.VMEM((rows, block, lanes), bf16),
-            dma((2, depth)), dma((2, depth)),
+            pltpu.VMEM((halves, block, wide), bf16),
+            pltpu.VMEM((halves, block, wide), bf16),
+            pltpu.VMEM((channels, 8), f32),
+            dma((2, 2, depth)), dma((2, depth)),
             dma((2, rows)), dma((2, rows)),
             dma((rows,)), dma((rows,)),
             dma((rows,)), dma((rows,)),
@@ -392,7 +444,8 @@
         compiler_params=pltpu.CompilerParams(collective_id=0, has_side_effects=True),
     )(
         latent.reshape(lanes, channels), hidden.reshape(lanes, channels),
-        cotangent.reshape(lanes, channels), f1, f2, params,
+        cotangent.reshape(lanes, channels), filter_one, filter_two,
+        *(vector.reshape(1, channels) for vector in (gain_one, shift_one, gain_two, shift_two)),
     )
     return out.reshape(latent.shape)
 
@@ -416,7 +469,8 @@
         fits = (
             rows_here == 1
             and images * breadth == 128
-            and rows % (2 * depth) == 0
+            and rows == 2 * depth
+            and rows % 2 == 0
             and channels % (rows * GSIZE) == 0
             and (channels // rows) % 16 == 0
             and channels % 128 == 0

time: 86.5 us -> 71 us (0.82)
  the two profiles are of different devices: /device:TPU:15 before, /device:TPU:0 now
where the time goes in v2:
time: 71 us; the launch traced here: 70.8 us
  Pallas kernels  66 us (93%)
  local copies, waits for them, and re-layouts  4.81 us (7%)
    pallas_call x1, Pallas kernels, kernel_body(): pl.pallas_call(functools.partial(kernel, depth, rows, breadth), out_shape...  66 us
    unnamed x9, local copies, waits for them, and re-layouts  2.5 us
    reshape x4, local copies, waits for them, and re-layouts, kernel_body(): vector.reshape(1, channels)  2.32 us

profile of v2, /device:TPU:0, one launch (start us, length us, event | category | flops | bytes accessed | tf_op | source)
XLA Modules:
  0.0 70.8 jit_solution(1300464545285128565)
XLA Ops:
  0.0 0.0 copy-start
  0.0 0.0 copy-start.1
  0.0 0.7 copy-done
  0.7 0.6 reshape.27.gain1
  1.3 0.0 copy-done.1
  1.3 0.0 copy-start.2
  1.3 0.6 reshape.28.shift1
  1.9 0.1 copy-done.2
  2.0 0.0 copy-start.3
  2.0 0.6 reshape.29.gain2
  2.5 0.1 copy-done.3
  2.7 0.6 reshape.30.shift2
  3.2 66.0 %shard_map.91 = bf16[128,640]{1,0:T(8,128)(2,1)} custom-call(bf16[128,640]{1,0:T(8,128)(2,1)} %bitcast.7, bf16[128,640]{1,0:T(8,128)(2,1)} %bitcast.8, bf16[128,640]{1,0:T(8,128)(2,1)} %bitcast.9, bf16[9,160,80]{2,1,0:T(8,128)(2,1)} %raw1.1, bf16[9,160,80]{2,1,0:T(8,128)(2,1)} %raw2.1, f32[1,640]{1,0:T(1,128)} %reshape.27.gain1, f32[1,640]{1,0:T(1,128)} %reshape.28.shift1, ...), custom_call_target="tpu_custom_call" | custom-call | tf_op jit(solution)/shard_map/pallas_call | solution.py:413
  69.2 1.6 %copy.12 = bf16[2,1,64,640]{3,2,1,0:T(8,128)(2,1)} copy(bf16[2,1,64,640]{3,2,1,0:T(8,128)(2,1)} %bitcast.6) | data formatting | bytes 327680
Async XLA Ops:
  0.0 0.7 copy-start
  0.0 1.3 %copy-start.1 = (f32[640]{0:T(1024)S(1)}, f32[640]{0:T(1024)}, u32[]{:S(2)}) copy-start(f32[640]{0:T(1024)} %param.15) | copy-start | bytes 7684
  1.3 0.7 copy-start.2
  2.0 0.7 copy-start.3

commit v3 on v2

--- a/solution.py
+++ b/solution.py
@@ -150,28 +150,32 @@
 
     pending = []
 
-    def z_hop(which, src, stage, origin, way):
+    def z_hop(which, src, stage, origin, k, way):
         to = d + 1 - 2 * way
-        return remote(src, stage.at[origin], z_send.at[which, way, origin], z_recv.at[which, origin], dp=to)
+        return remote(
+            src, stage.at[origin, k], z_send.at[which, way, origin, k], z_recv.at[which, origin, k], dp=to
+        )
 
     def start_z(which, src, stage):
-        @pl.when(d < depth - 1)
-        def _():
-            z_hop(which, src, stage, d, 0).start()
-
-        @pl.when(d > 0)
-        def _():
-            z_hop(which, src, stage, d, 1).start()
+        for k in range(halves):
+            @pl.when(d < depth - 1)
+            def _():
+                z_hop(which, src.at[k], stage, d, k, 0).start()
+
+            @pl.when(d > 0)
+            def _():
+                z_hop(which, src.at[k], stage, d, k, 1).start()
 
     def wait_z_sends(which, src, stage):
         for origin in range(depth):
-            @pl.when((d < depth - 1) & (origin <= d))
-            def _():
-                z_hop(which, src, stage, origin, 0).wait_send()
-
-            @pl.when((d > 0) & (origin >= d))
-            def _():
-                z_hop(which, src, stage, origin, 1).wait_send()
+            for k in range(halves):
+                @pl.when((d < depth - 1) & (origin <= d))
+                def _():
+                    z_hop(which, src.at[k], stage, origin, k, 0).wait_send()
+
+                @pl.when((d > 0) & (origin >= d))
+                def _():
+                    z_hop(which, src.at[k], stage, origin, k, 1).wait_send()
 
     def start_exchange(which, src, dst):
         for off in range(1, rows):
@@ -189,17 +193,20 @@
             frm = lax.rem(r + off, rows)
             remote(src.at[pl.ds(0, block), :], dst.at[frm], a_send.at[which, frm], a_recv.at[which, frm], rows=frm).wait_recv()
 
-    def send_pieces(which, origin, get, w, wait_own):
+    def send_piece(which, origin, k, piece, w):
+        to = place(origin * halves + k)
+
+        @pl.when(to != r)
+        def _():
+            remote(piece, w.at[r], w_send.at[which, to], w_recv.at[which, r], rows=to).start()
+
+        @pl.when(to == r)
+        def _():
+            w[r] = piece[...]
+
+    def send_own(which, src, w):
         for k in range(halves):
-            to = place(origin * halves + k)
-
-            @pl.when(to != r)
-            def _():
-                remote(get(k), w.at[r], w_send.at[which, to], w_recv.at[which, r], rows=to).start()
-
-            @pl.when(to == r)
-            def _():
-                w[r] = get(k)[...]
+            send_piece(which, d, k, src.at[k], w)
 
     def wait_piece_sends(which, src, w):
         for off in range(1, rows):
@@ -207,29 +214,20 @@
             remote(src.at[0], w.at[r], w_send.at[which, to], w_recv.at[which, r], rows=to).wait_send()
 
     def relay_filters(which, stage, w, off):
-        @pl.when(d >= off)
-        def _():
-            origin = d - off
-            hop = z_hop(which, stage.at[origin], stage, origin, 0)
-            hop.wait_recv()
-
-            @pl.when(d < depth - 1)
-            def _():
-                hop.start()
-
-            send_pieces(which, origin, lambda k: stage.at[origin, k], w, False)
-
-        @pl.when(d + off < depth)
-        def _():
-            origin = d + off
-            hop = z_hop(which, stage.at[origin], stage, origin, 1)
-            hop.wait_recv()
-
-            @pl.when(d > 0)
-            def _():
-                hop.start()
-
-            send_pieces(which, origin, lambda k: stage.at[origin, k], w, False)
+        for k in range(halves):
+            for way in range(2):
+                origin = d - off if way == 0 else d + off
+
+                @pl.when((origin >= 0) & (origin < depth))
+                def _():
+                    hop = z_hop(which, stage.at[origin, k], stage, origin, k, way)
+                    hop.wait_recv()
+
+                    @pl.when((d < depth - 1) if way == 0 else (d > 0))
+                    def _():
+                        hop.start()
+
+                    send_piece(which, origin, k, stage.at[origin, k], w)
 
     def wait_filters(which, src, w):
         for off in range(1, rows):
@@ -272,10 +270,9 @@
     start_z(0, f2_ref, stage2)
     gather_send(cot_at, c_send, c_recv)
     start_exchange(0, hid_t, hid_b)
-    send_pieces(0, d, lambda k: f2_ref.at[k], w2, True)
-    start_exchange(1, lat_t, lat_b)
+    send_own(0, f2_ref, w2)
     arrange(raw1, f1_ref)
-    raw_params = [gain1[...], shift1[...], gain2[...], shift2[...]]
+    raw_params = [p[...].reshape(1, channels) for p in (gain1, shift1, gain2, shift2)]
     par_ref[...] = jnp.concatenate(raw_params + raw_params, axis=0).T
 
     lane = lax.broadcasted_iota(jnp.int32, (1, lanes), 1)
@@ -347,30 +344,33 @@
             normed = (field[h].astype(jnp.float32) - average) * inverse
             finish(h, inverse * (back[h] - first - normed * second))
 
+    relay_filters(0, stage2, w2, 1)
     gather_relay(cot_at, c_send, c_recv)
-    relay_filters(0, stage2, w2, 1)
+    start_exchange(1, lat_t, lat_b)
+    relay_filters(0, stage2, w2, 2)
     wait_exchange(0, hid_t, hid_b)
     moments_two = stats(hid_b)
+    start_z(1, f1_ref, stage1)
+    for off in range(3, depth):
+        relay_filters(0, stage2, w2, off)
+    gather_wait(cot_at, c_send, c_recv)
+    wait_filters(0, f2_ref, w2)
+
+    conv(x_cot, w2)
+    send_own(1, f1_ref, w1)
+    relay_filters(1, stage1, w1, 1)
+    mine = rows_of(r)
+
+    def finish_two(h, value):
+        x_hg[h, mine, :] = value.astype(jnp.bfloat16)
+
+    norm(hid_b, moments_two, params[:, 2:3], params[:, 3:4], finish_two)
+    gather_send(hg_at, g_send, g_recv)
     wait_exchange(1, lat_t, lat_b)
     moments_one = stats(lat_b)
-    for off in range(2, depth):
-        relay_filters(0, stage2, w2, off)
-    start_z(1, f1_ref, stage1)
-    gather_wait(cot_at, c_send, c_recv)
-    wait_filters(0, f2_ref, w2)
-
-    conv(x_cot, w2)
-    mine = rows_of(r)
-
-    def finish_two(h, value):
-        x_hg[h, mine, :] = value.astype(jnp.bfloat16)
-
-    norm(hid_b, moments_two, params[:, 2:3], params[:, 3:4], finish_two)
-    gather_send(hg_at, g_send, g_recv)
-    send_pieces(1, d, lambda k: f1_ref.at[k], w1, True)
-    relay_filters(1, stage1, w1, 1)
+    relay_filters(1, stage1, w1, 2)
     gather_relay(hg_at, g_send, g_recv)
-    for off in range(2, depth):
+    for off in range(3, depth):
         relay_filters(1, stage1, w1, off)
     gather_wait(hg_at, g_send, g_recv)
     wait_filters(1, f1_ref, w1)
@@ -434,7 +434,7 @@
             pltpu.VMEM((halves, block, wide), bf16),
             pltpu.VMEM((halves, block, wide), bf16),
             pltpu.VMEM((channels, 8), f32),
-            dma((2, 2, depth)), dma((2, depth)),
+            dma((2, 2, depth, halves)), dma((2, depth, halves)),
             dma((2, rows)), dma((2, rows)),
             dma((rows,)), dma((rows,)),
             dma((rows,)), dma((rows,)),
@@ -445,7 +445,7 @@
     )(
         latent.reshape(lanes, channels), hidden.reshape(lanes, channels),
         cotangent.reshape(lanes, channels), filter_one, filter_two,
-        *(vector.reshape(1, channels) for vector in (gain_one, shift_one, gain_two, shift_two)),
+        gain_one, shift_one, gain_two, shift_two,
     )
     return out.reshape(latent.shape)
 
@@ -469,6 +469,7 @@
         fits = (
             rows_here == 1
             and images * breadth == 128
+            and depth > 2
             and rows == 2 * depth
             and rows % 2 == 0
             and channels % (rows * GSIZE) == 0

time: 71 us -> 60.4 us (0.85)
  Pallas kernels: 66 us -> 58.7 us
  local copies, waits for them, and re-layouts: 4.81 us -> 1.6 us
    pallas_call x1, Pallas kernels: 66 us -> 58.7 us  [kernel_body(): pl.pallas_call(functools.partial(kernel, depth, rows, breadth), out_shape...]
    reshape x4 -> x0, local copies, waits for them, and re-layouts: 2.32 us -> none  [kernel_body(): vector.reshape(1, channels)]
    unnamed x9 -> x1, local copies, waits for them, and re-layouts: 2.5 us -> 1.6 us
where the time goes in v3:
time: 60.4 us; the launch traced here: 60.3 us
  Pallas kernels  58.7 us (97%)
  local copies, waits for them, and re-layouts  1.6 us (3%)
    pallas_call x1, Pallas kernels, kernel_body(): pl.pallas_call(functools.partial(kernel, depth, rows, breadth), out_shape...  58.7 us
    unnamed x1, local copies, waits for them, and re-layouts  1.6 us

profile of v3, /device:TPU:0, one launch (start us, length us, event | category | flops | bytes accessed | tf_op | source)
XLA Modules:
  0.0 60.3 jit_solution(10267156022839915444)
XLA Ops:
  0.0 58.7 %shard_map.91 = bf16[128,640]{1,0:T(8,128)(2,1)} custom-call(bf16[128,640]{1,0:T(8,128)(2,1)} %bitcast.7, bf16[128,640]{1,0:T(8,128)(2,1)} %bitcast.8, bf16[128,640]{1,0:T(8,128)(2,1)} %bitcast.9, bf16[9,160,80]{2,1,0:T(8,128)(2,1)} %raw1.1, bf16[9,160,80]{2,1,0:T(8,128)(2,1)} %raw2.1, f32[640]{0:T(1024)} %gain1.1, f32[640]{0:T(1024)} %shift1.1, f32[640]{0:T(1024)} %gain2.1, ...), custom_call_target="tpu_custom_call" | custom-call | tf_op jit(solution)/shard_map/pallas_call | solution.py:413
  58.7 1.6 %copy.12 = bf16[2,1,64,640]{3,2,1,0:T(8,128)(2,1)} copy(bf16[2,1,64,640]{3,2,1,0:T(8,128)(2,1)} %bitcast.6) | data formatting | bytes 327680

commit v4 on v3

--- a/solution.py
+++ b/solution.py
@@ -369,9 +369,9 @@
     wait_exchange(1, lat_t, lat_b)
     moments_one = stats(lat_b)
     relay_filters(1, stage1, w1, 2)
-    gather_relay(hg_at, g_send, g_recv)
     for off in range(3, depth):
         relay_filters(1, stage1, w1, off)
+    gather_relay(hg_at, g_send, g_recv)
     gather_wait(hg_at, g_send, g_recv)
     wait_filters(1, f1_ref, w1)
 

time: 60.4 us -> 58.7 us (0.972)
  Pallas kernels: 58.7 us -> 56.9 us
    pallas_call x1, Pallas kernels: 58.7 us -> 56.9 us  [kernel_body(): pl.pallas_call(functools.partial(kernel, depth, rows, breadth), out_shape...]
where the time goes in v4:
time: 58.7 us; the launch traced here: 58.5 us
  Pallas kernels  56.9 us (97%)
  local copies, waits for them, and re-layouts  1.6 us (3%)
    pallas_call x1, Pallas kernels, kernel_body(): pl.pallas_call(functools.partial(kernel, depth, rows, breadth), out_shape...  56.9 us
    unnamed x1, local copies, waits for them, and re-layouts  1.6 us

profile of v4, /device:TPU:0, one launch (start us, length us, event | category | flops | bytes accessed | tf_op | source)
XLA Modules:
  0.0 58.5 jit_solution(16518307797098665622)
XLA Ops:
  0.0 56.9 %shard_map.91 = bf16[128,640]{1,0:T(8,128)(2,1)} custom-call(bf16[128,640]{1,0:T(8,128)(2,1)} %bitcast.7, bf16[128,640]{1,0:T(8,128)(2,1)} %bitcast.8, bf16[128,640]{1,0:T(8,128)(2,1)} %bitcast.9, bf16[9,160,80]{2,1,0:T(8,128)(2,1)} %raw1.1, bf16[9,160,80]{2,1,0:T(8,128)(2,1)} %raw2.1, f32[640]{0:T(1024)} %gain1.1, f32[640]{0:T(1024)} %shift1.1, f32[640]{0:T(1024)} %gain2.1, ...), custom_call_target="tpu_custom_call" | custom-call | tf_op jit(solution)/shard_map/pallas_call | solution.py:413
  56.9 1.6 %copy.12 = bf16[2,1,64,640]{3,2,1,0:T(8,128)(2,1)} copy(bf16[2,1,64,640]{3,2,1,0:T(8,128)(2,1)} %bitcast.6) | data formatting | bytes 327680
